TPU v7x, 32 devices: a whole 2x2x4 slice. The times are simulated.
32 devices in a mesh: gx: 2 (over x), gy: 4 (over z), gz: 4 (over y, core).
Axes of the slice: x: 2, y: 2, z: 4, core: 2. Of those that a mesh axis runs over, the one named last changes fastest.
Arguments:
- fields: float32 [4, 8, 256, 512], P(None, 'gx', 'gy', 'gz'), may hold values from -8 to 8
- volume_code: int32 [8, 256, 512], P('gx', 'gy', 'gz'), may hold values from 65536 to 1048576
- cut_flag: int32 [8, 256, 512], P('gx', 'gy', 'gz'), may hold values 0 or 1
- member_bits: int32 [8, 256, 512], P('gx', 'gy', 'gz'), may hold values from 0 to 134217727
Outputs:
- merged: float32 [4, 8, 256, 512], P(None, 'gx', 'gy', 'gz')
All inputs are finite; a program needn't handle non-finite values. No bound on the sum of `cut_flag` on one device may be relied on, other than what follows from the above.
Results may differ from a plain program's by a relative error of at most 0.00015.
Values sent between devices are 32-bit elements; how exact they have to be, the bound alone decides.
A program may use at most 128 MiB of HBM per device.

v0:
```python
import jax
import jax.numpy as jnp
from jax import lax
from jax.sharding import PartitionSpec as P

PASSES = 2


def extended(block, sides, width):
    for axis, dim in sides:
        count = lax.axis_size(axis)
        forward = [(i, i + 1) for i in range(count - 1)]
        forward.append((count - 1, 0))
        backward = [(target, source) for source, target in forward]
        low = lax.ppermute(
            lax.slice_in_dim(block, block.shape[dim] - width, None, axis=dim), axis, forward
        )
        high = lax.ppermute(lax.slice_in_dim(block, 0, width, axis=dim), axis, backward)
        block = jnp.concatenate([low, block, high], axis=dim)
    return block


def offset_list():
    result = []
    for dx in (-1, 0, 1):
        for dy in (-1, 0, 1):
            for dz in (-1, 0, 1):
                result.append((dx, dy, dz))
    return result


def member_bit(active, index):
    return jnp.bitwise_and(jnp.right_shift(active, index), 1).astype(jnp.float32)


def pulled_sums(padded, offsets, sizex, sizey, sizez):
    sums = jnp.zeros((5, sizex, sizey, sizez), jnp.float32)
    for index, shift in enumerate(offsets):
        dx, dy, dz = shift
        piece = padded[:, 1 - dx : 1 - dx + sizex, 1 - dy : 1 - dy + sizey, 1 - dz : 1 - dz + sizez]
        if index == 13:
            sums = sums + piece[:5]
        else:
            if index < 14:
                member = member_bit(piece[5].astype(jnp.int32), index)
            else:
                member = member_bit(piece[6].astype(jnp.int32), index - 14)
            sums = sums + member[None] * piece[:5]
    return sums


def body(fields, volume_code, cut_flag, member_bits):
    sizex, sizey, sizez = volume_code.shape
    kappa = volume_code.astype(jnp.float32) / 1048576.0
    active = member_bits * cut_flag
    offsets = offset_list()
    own_bits = []
    count = jnp.zeros_like(kappa)
    for index in range(27):
        if index == 13:
            member = jnp.ones_like(kappa)
        else:
            member = member_bit(active, index)
        own_bits.append(member)
        count = count + member
    low_part = jnp.bitwise_and(active, 16383).astype(jnp.float32)
    high_part = jnp.right_shift(active, 14).astype(jnp.float32)
    state = fields
    for step in range(PASSES):
        weighted = kappa[None] * state
        packed = jnp.concatenate([kappa[None], weighted, low_part[None], high_part[None]], axis=0)
        padded = extended(packed, (("gx", 1), ("gy", 2), ("gz", 3)), 1)
        sums = pulled_sums(padded, offsets, sizex, sizey, sizez)
        hat = sums[1:] / sums[0:1]
        framed = extended(hat, (("gx", 1), ("gy", 2), ("gz", 3)), 1)
        total = jnp.zeros_like(state)
        for index, shift in enumerate(offsets):
            dx, dy, dz = shift
            piece = framed[
                :, 1 + dx : 1 + dx + sizex, 1 + dy : 1 + dy + sizey, 1 + dz : 1 + dz + sizez
            ]
            total = total + own_bits[index][None] * piece
        state = total / count[None]
    return state


def solution(mesh):
    in_specs = (
        P(None, "gx", "gy", "gz"),
        P("gx", "gy", "gz"),
        P("gx", "gy", "gz"),
        P("gx", "gy", "gz"),
    )
    out_specs = P(None, "gx", "gy", "gz")
    return jax.shard_map(body, mesh=mesh, in_specs=in_specs, out_specs=out_specs, check_vma=False)
```

profile of v0, /device:TPU:0, one launch (start us, length us, event | category | flops | bytes accessed | tf_op | source)
XLA Modules:
  0.0 150.6 jit_solution(13559110110422947061)
XLA Ops:
  0.0 0.9 convert_multiply_fusion
  0.9 1.7 %and_convert_fusion.25 = (f32[4,64,128]{2,1,0:T(8,128)}, s32[4,64,128]{2,1,0:T(8,128)S(1)}) fusion(s32[4,64,128]{2,1,0:T(8,128)} %param.7, s32[4,64,128]{2,1,0:T(8,128)} %param.6), kind=kLoop, calls=%fused_computation.623 | loop fusion | flops 131072 | bytes 524288 | tf_op jit(solution)/shard_map/convert_element_type | solution.py:33
  2.6 1.7 %and_convert_fusion.24 = (f32[4,64,128]{2,1,0:T(8,128)}, f32[4,64,128]{2,1,0:T(8,128)}, f32[4,64,128]{2,1,0:T(8,128)}, f32[4,64,128]{2,1,0:T(8,128)}, f32[4,64,1...) fusion(s32[4,64,128]{2,1,0:T(8,128)S(1)} %get-tuple-element.6), kind=kLoop, calls=%fused_computation.619 | loop fusion | flops 2555904 | bytes 3670016 | tf_op jit(solution)/shard_map/convert_element_type | solution.py:33
  4.6 3.0 %collective-permute-start = (f32[7,1,64,128]{3,2,1,0:T(8,128)S(1)}, f32[7,1,64,128]{3,2,1,0:T(8,128)S(1)}, u32[]{:S(2)}, u32[]{:S(2)}) collective-permute-start(f32[7,1,64,128]{3,2,1,0:T(8,128)S(1)} %get-tuple-element.77), channel_id=1, source_target_pairs={{0,16},{16,0},{1,17},{17,1},{2,18},{18,2},{3,19},{19,3},{4,20},{20... | collective-permute-start | bytes 688136 | tf_op jit(solution)/shard_map/ppermute | solution.py:15
  7.7 6.4 %collective-permute-done = f32[7,1,64,128]{3,2,1,0:T(8,128)S(1)} collective-permute-done((f32[7,1,64,128]{3,2,1,0:T(8,128)S(1)}, f32[7,1,64,128]{3,2,1,0:T(8,128)S(1)}, u32[]{:S(2)}, u32[]{:S(2)}) %collective-permute-start) | collective-permute-done | bytes 229408 | tf_op jit(solution)/shard_map/ppermute | solution.py:15
  14.1 4.1 %collective-permute-done.1 = f32[7,1,64,128]{3,2,1,0:T(8,128)S(1)} collective-permute-done((f32[7,1,64,128]{3,2,1,0:T(8,128)S(1)}, f32[7,1,64,128]{3,2,1,0:T(8,128)S(1)}, u32[]{:S(2)}, u32[]{:S(2)}) %collective-permute-start.1) | collective-permute-done | bytes 229408 | tf_op jit(solution)/shard_map/ppermute | solution.py:18
  18.3 3.9 %collective-permute-start.3 = (f32[7,6,1,128]{3,0,2,1:T(8,128)S(1)}, f32[7,6,1,128]{3,0,2,1:T(8,128)S(1)}, u32[]{:S(2)}, u32[]{:S(2)}) collective-permute-start(f32[7,6,1,128]{3,0,2,1:T(8,128)S(1)} %copy.335), channel_id=1, source_target_pairs={{4,0},{8,4},{12,8},{0,12},{5,1},{9,5},{13,9},{1,13},{6,2},{10,6},{... | collective-permute-start | bytes 64520 | tf_op jit(solution)/shard_map/ppermute | solution.py:18
  22.5 0.8 fusion.282
  23.7 4.1 %collective-permute-done.2 = f32[7,6,1,128]{3,0,2,1:T(8,128)S(1)} collective-permute-done((f32[7,6,1,128]{3,0,2,1:T(8,128)S(1)}, f32[7,6,1,128]{3,0,2,1:T(8,128)S(1)}, u32[]{:S(2)}, u32[]{:S(2)}) %collective-permute-start.2) | collective-permute-done | bytes 21536 | tf_op jit(solution)/shard_map/ppermute | solution.py:15
  28.1 1.6 %fusion.369 = (f32[7,6,66,1]{3,2,1,0:T(8,128)}, f32[7,6,66,1]{3,2,1,0:T(8,128)S(1)}) fusion(f32[7,6,66,128]{3,2,1,0:T(8,128)S(1)} %fusion.35), kind=kLoop, calls=%fused_computation.632 | loop fusion | bytes 44352 | tf_op jit(solution)/shard_map/slice | solution.py:18
  29.7 2.6 %copy.298 = f32[7,6,66,1]{2,0,3,1:T(8,128)} copy(f32[7,6,66,1]{3,2,1,0:T(8,128)} %get-tuple-element.57) | data formatting | bytes 22176 | tf_op jit(solution)/shard_map/slice | solution.py:18
  32.3 0.6 copy.301
  33.0 1.7 %collective-permute-start.4 = (f32[7,6,66,1]{2,0,3,1:T(8,128)}, f32[7,6,66,1]{2,0,3,1:T(8,128)}, u32[]{:S(2)}, u32[]{:S(2)}) collective-permute-start(f32[7,6,66,1]{2,0,3,1:T(8,128)} %copy.298), channel_id=1, source_target_pairs={{1,0},{2,1},{3,2},{0,3},{5,4},{6,5},{7,6},{4,7},{9,8},{10,9},{11,1... | collective-permute-start | bytes 33272 | tf_op jit(solution)/shard_map/ppermute | solution.py:18
  35.0 1.1 copy-done.2
  36.1 0.9 fusion.338
  37.0 2.5 %copy.299 = f32[7,6,66,1]{3,2,1,0:T(8,128)} copy(f32[7,6,66,1]{2,0,3,1:T(8,128)} %collective-permute-done.4) | data formatting | bytes 22176 | tf_op jit(solution)/shard_map/ppermute | solution.py:18
  39.5 1.8 %copy.302 = f32[7,6,66,1]{3,2,1,0:T(8,128)} copy(f32[7,6,66,1]{2,0,3,1:T(8,128)S(1)} %collective-permute-done.5) | data formatting | bytes 22176 | tf_op jit(solution)/shard_map/ppermute | solution.py:15
  41.2 6.1 %fusion.14 = (f32[7,6,66,129]{3,2,1,0:T(8,128)S(1)}, f32[7,6,66,129]{3,2,1,0:T(8,128)S(1)}) fusion(f32[1,4,64,128]{3,2,1,0:T(8,128)S(1)} %get-tuple-element.124, f32[1,4,64,128]{3,2,1,0:T(8,128)S(1)} %get-tuple-element.125, f32[1,4,64,128]{3,2,1,0:T(8,128)S(1)} %get-tuple-element.127, f32[7,6,66,1]{3,2,1,0:T(8,128)} %copy.299, ...), kind=kLoop, calls=%fused_computation.26 | loop fusion | flops 5721408 | bytes 4302144 | tf_op jit(solution)/shard_map/concatenate | solution.py:19
  47.5 0.6 fusion.358
  48.0 0.8 copy-done.3
  49.6 2.9 %fusion.61 = f32[5,4,64,128]{3,2,1,0:T(8,128)S(1)} fusion(f32[1,4,64,128]{3,2,1,0:T(8,128)S(1)} %get-tuple-element.127, f32[7,6,66,129]{3,2,1,0:T(8,128)S(1)} %get-tuple-element.62, f32[7,6,65,128]{3,2,1,0:T(8,128)S(1)} %copy-done.3, f32[7,6,66,129]{3,2,1,0:T(8,128)S(1)} %get-tuple-element.61, f32[7,5,64,128]{3,2,1,0:T(8,128)S(1)} %copy-done.11, ...), kind=kLoop, calls=%fused_computation.127 | loop fusion | flops 8683520 | bytes 21757952 | tf_op jit(solution)/shard_map/add | solution.py:48
  52.6 1.6 %collective-permute-start.6 = (f32[4,1,64,128]{3,2,1,0:T(8,128)S(1)}, f32[4,1,64,128]{3,2,1,0:T(8,128)S(1)}, u32[]{:S(2)}, u32[]{:S(2)}) collective-permute-start(f32[4,1,64,128]{3,2,1,0:T(8,128)S(1)} %get-tuple-element.97), channel_id=1, source_target_pairs={{0,16},{16,0},{1,17},{17,1},{2,18},{18,2},{3,19},{19,3},{4,20},{20... | collective-permute-start | bytes 393224 | tf_op jit(solution)/shard_map/ppermute | solution.py:15
  54.2 0.5 collective-permute-start.7
  54.7 4.1 %collective-permute-done.6 = f32[4,1,64,128]{3,2,1,0:T(8,128)S(1)} collective-permute-done((f32[4,1,64,128]{3,2,1,0:T(8,128)S(1)}, f32[4,1,64,128]{3,2,1,0:T(8,128)S(1)}, u32[]{:S(2)}, u32[]{:S(2)}) %collective-permute-start.6) | collective-permute-done | bytes 131104 | tf_op jit(solution)/shard_map/ppermute | solution.py:15
  58.9 2.8 %collective-permute-done.7 = f32[4,1,64,128]{3,2,1,0:T(8,128)S(1)} collective-permute-done((f32[4,1,64,128]{3,2,1,0:T(8,128)S(1)}, f32[4,1,64,128]{3,2,1,0:T(8,128)S(1)}, u32[]{:S(2)}, u32[]{:S(2)}) %collective-permute-start.7) | collective-permute-done | bytes 131104 | tf_op jit(solution)/shard_map/ppermute | solution.py:18
  61.8 2.0 %collective-permute-start.8 = (f32[4,6,1,128]{3,1,2,0:T(8,128)S(1)}, f32[4,6,1,128]{3,1,2,0:T(8,128)S(1)}, u32[]{:S(2)}, u32[]{:S(2)}) collective-permute-start(f32[4,6,1,128]{3,1,2,0:T(8,128)S(1)} %copy.304), channel_id=1, source_target_pairs={{0,4},{4,8},{8,12},{12,0},{1,5},{5,9},{9,13},{13,1},{2,6},{6,10},{... | collective-permute-start | bytes 36872 | tf_op jit(solution)/shard_map/ppermute | solution.py:15
  63.8 1.1 add_add_fusion
  64.9 0.6 collective-permute-done.9
  65.5 1.8 %collective-permute-done.8 = f32[4,6,1,128]{3,1,2,0:T(8,128)S(1)} collective-permute-done((f32[4,6,1,128]{3,1,2,0:T(8,128)S(1)}, f32[4,6,1,128]{3,1,2,0:T(8,128)S(1)}, u32[]{:S(2)}, u32[]{:S(2)}) %collective-permute-start.8) | collective-permute-done | bytes 12320 | tf_op jit(solution)/shard_map/ppermute | solution.py:15
  69.3 2.8 %collective-permute-done.10 = f32[4,6,66,1]{2,1,3,0:T(8,128)S(1)} collective-permute-done((f32[4,6,66,1]{2,1,3,0:T(8,128)S(1)}, f32[4,6,66,1]{2,1,3,0:T(8,128)S(1)}, u32[]{:S(2)}, u32[]{:S(2)}) %collective-permute-start.10) | collective-permute-done | bytes 6368 | tf_op jit(solution)/shard_map/ppermute | solution.py:15
  72.1 1.3 copy.309
  73.4 1.3 copy.312
  74.9 2.4 %maximum_maximum_fusion = (f32[4,6,66,129]{3,2,1,0:T(8,128)S(1)}, f32[4,6,66,129]{3,2,1,0:T(8,128)S(1)}) fusion(f32[4,6,1,128]{3,2,1,0:T(1,128)S(1)} %copy.307, f32[4,1,64,128]{3,2,1,0:T(8,128)S(1)} %collective-permute-done.7, f32[4,4,64,128]{3,2,1,0:T(8,128)S(1)} %slice_divide_fusion.1, f32[4,1,64,128]{3,2,1,0:T(8,128)S(1)} %collective-permute-done.6, ...), kind=kLoop, calls=%fused_computation.56 | loop fusion | flops 2043360 | bytes 2458368 | tf_op jit(solution)/shard_map/concatenate | solution.py:19
  77.6 2.6 %fusion.131 = f32[4,4,64,128]{3,2,1,0:T(8,128)S(1)} fusion(f32[4,6,66,129]{3,2,1,0:T(8,128)S(1)} %get-tuple-element.86, f32[4,6,65,128]{3,2,1,0:T(8,128)S(1)} %get-tuple-element.92, f32[4,6,66,129]{3,2,1,0:T(8,128)S(1)} %get-tuple-element.85, f32[4,1,64,128]{3,2,1,0:T(8,128)S(1)} %collective-permute-done.7, f32[4,4,64,128]{3,2,1,0:T(8,128)S(1)} %slice_divide_fusion.1, ...), kind=kLoop, calls=%fused_computation.277 | loop fusion | flops 7340032 | bytes 17563648 | tf_op jit(solution)/shard_map/mul | solution.py:70
  80.4 1.6 %collective-permute-start.12 = (f32[7,1,64,128]{3,2,1,0:T(8,128)S(1)}, f32[7,1,64,128]{3,2,1,0:T(8,128)S(1)}, u32[]{:S(2)}, u32[]{:S(2)}) collective-permute-start(f32[7,1,64,128]{3,2,1,0:T(8,128)S(1)} %get-tuple-element.73), channel_id=1, source_target_pairs={{0,16},{16,0},{1,17},{17,1},{2,18},{18,2},{3,19},{19,3},{4,20},{20... | collective-permute-start | bytes 688136 | tf_op jit(solution)/shard_map/ppermute | solution.py:15
  81.9 0.5 collective-permute-start.13
  82.4 6.5 %collective-permute-done.12 = f32[7,1,64,128]{3,2,1,0:T(8,128)S(1)} collective-permute-done((f32[7,1,64,128]{3,2,1,0:T(8,128)S(1)}, f32[7,1,64,128]{3,2,1,0:T(8,128)S(1)}, u32[]{:S(2)}, u32[]{:S(2)}) %collective-permute-start.12) | collective-permute-done | bytes 229408 | tf_op jit(solution)/shard_map/ppermute | solution.py:15
  88.9 2.7 %collective-permute-done.13 = f32[7,1,64,128]{3,2,1,0:T(8,128)S(1)} collective-permute-done((f32[7,1,64,128]{3,2,1,0:T(8,128)S(1)}, f32[7,1,64,128]{3,2,1,0:T(8,128)S(1)}, u32[]{:S(2)}, u32[]{:S(2)}) %collective-permute-start.13) | collective-permute-done | bytes 229408 | tf_op jit(solution)/shard_map/ppermute | solution.py:18
  92.0 1.9 %collective-permute-start.14 = (f32[7,6,1,128]{3,0,2,1:T(8,128)S(1)}, f32[7,6,1,128]{3,0,2,1:T(8,128)S(1)}, u32[]{:S(2)}, u32[]{:S(2)}) collective-permute-start(f32[7,6,1,128]{3,0,2,1:T(8,128)S(1)} %copy.336), channel_id=1, source_target_pairs={{0,4},{4,8},{8,12},{12,0},{1,5},{5,9},{9,13},{13,1},{2,6},{6,10},{... | collective-permute-start | bytes 64520 | tf_op jit(solution)/shard_map/ppermute | solution.py:15
  94.2 1.4 collective-permute-done.15
  95.7 1.9 %collective-permute-done.14 = f32[7,6,1,128]{3,0,2,1:T(8,128)S(1)} collective-permute-done((f32[7,6,1,128]{3,0,2,1:T(8,128)S(1)}, f32[7,6,1,128]{3,0,2,1:T(8,128)S(1)}, u32[]{:S(2)}, u32[]{:S(2)}) %collective-permute-start.14) | collective-permute-done | bytes 21536 | tf_op jit(solution)/shard_map/ppermute | solution.py:15
  97.8 1.6 %fusion.368 = (f32[7,6,66,1]{3,2,1,0:T(8,128)}, f32[7,6,66,1]{3,2,1,0:T(8,128)S(1)}) fusion(f32[7,6,66,128]{3,2,1,0:T(8,128)S(1)} %fusion.39), kind=kLoop, calls=%fused_computation.631 | loop fusion | bytes 44352 | tf_op jit(solution)/shard_map/slice | solution.py:18
  99.5 2.6 %copy.318 = f32[7,6,66,1]{2,0,3,1:T(8,128)} copy(f32[7,6,66,1]{3,2,1,0:T(8,128)} %get-tuple-element.49) | data formatting | bytes 22176 | tf_op jit(solution)/shard_map/slice | solution.py:18
  102.1 0.6 copy.321
  102.7 1.7 %collective-permute-start.16 = (f32[7,6,66,1]{2,0,3,1:T(8,128)}, f32[7,6,66,1]{2,0,3,1:T(8,128)}, u32[]{:S(2)}, u32[]{:S(2)}) collective-permute-start(f32[7,6,66,1]{2,0,3,1:T(8,128)} %copy.318), channel_id=1, source_target_pairs={{1,0},{2,1},{3,2},{0,3},{5,4},{6,5},{7,6},{4,7},{9,8},{10,9},{11,1... | collective-permute-start | bytes 33272 | tf_op jit(solution)/shard_map/ppermute | solution.py:18
  104.7 0.8 fusion.258
  105.9 0.8 fusion.234
  106.7 2.5 %copy.319 = f32[7,6,66,1]{3,2,1,0:T(8,128)} copy(f32[7,6,66,1]{2,0,3,1:T(8,128)} %collective-permute-done.16) | data formatting | bytes 22176 | tf_op jit(solution)/shard_map/ppermute | solution.py:18
  109.2 1.8 %copy.322 = f32[7,6,66,1]{3,2,1,0:T(8,128)} copy(f32[7,6,66,1]{2,0,3,1:T(8,128)S(1)} %collective-permute-done.17) | data formatting | bytes 22176 | tf_op jit(solution)/shard_map/ppermute | solution.py:15
  111.0 6.1 %fusion.19 = (f32[7,6,66,129]{3,2,1,0:T(8,128)S(1)}, f32[7,6,66,129]{3,2,1,0:T(8,128)S(1)}) fusion(f32[1,4,64,128]{3,2,1,0:T(8,128)S(1)} %get-tuple-element.124, f32[1,4,64,128]{3,2,1,0:T(8,128)S(1)} %get-tuple-element.125, f32[1,4,64,128]{3,2,1,0:T(8,128)S(1)} %get-tuple-element.127, f32[7,6,66,1]{3,2,1,0:T(8,128)} %copy.319, ...), kind=kLoop, calls=%fused_computation.31 | loop fusion | flops 5721408 | bytes 4302144 | tf_op jit(solution)/shard_map/concatenate | solution.py:19
  117.8 0.6 copy-done.5
  118.7 0.6 copy-done.1
  119.4 2.9 %fusion.75 = f32[5,4,64,128]{3,2,1,0:T(8,128)S(1)} fusion(f32[1,4,64,128]{3,2,1,0:T(8,128)S(1)} %get-tuple-element.127, f32[7,6,66,129]{3,2,1,0:T(8,128)S(1)} %get-tuple-element.60, f32[7,6,65,128]{3,2,1,0:T(8,128)S(1)} %copy-done.1, f32[7,6,66,129]{3,2,1,0:T(8,128)S(1)} %get-tuple-element.59, f32[7,5,64,128]{3,2,1,0:T(8,128)S(1)} %copy-done.7, ...), kind=kLoop, calls=%fused_computation.141 | loop fusion | flops 8683520 | bytes 21757952 | tf_op jit(solution)/shard_map/add | solution.py:48
  122.4 1.6 %collective-permute-start.18 = (f32[4,1,64,128]{3,2,1,0:T(8,128)S(1)}, f32[4,1,64,128]{3,2,1,0:T(8,128)S(1)}, u32[]{:S(2)}, u32[]{:S(2)}) collective-permute-start(f32[4,1,64,128]{3,2,1,0:T(8,128)S(1)} %get-tuple-element.95), channel_id=1, source_target_pairs={{0,16},{16,0},{1,17},{17,1},{2,18},{18,2},{3,19},{19,3},{4,20},{20... | collective-permute-start | bytes 393224 | tf_op jit(solution)/shard_map/ppermute | solution.py:15
  124.5 4.3 %collective-permute-done.18 = f32[4,1,64,128]{3,2,1,0:T(8,128)S(1)} collective-permute-done((f32[4,1,64,128]{3,2,1,0:T(8,128)S(1)}, f32[4,1,64,128]{3,2,1,0:T(8,128)S(1)}, u32[]{:S(2)}, u32[]{:S(2)}) %collective-permute-start.18) | collective-permute-done | bytes 131104 | tf_op jit(solution)/shard_map/ppermute | solution.py:15
  128.9 2.6 %collective-permute-done.19 = f32[4,1,64,128]{3,2,1,0:T(8,128)S(1)} collective-permute-done((f32[4,1,64,128]{3,2,1,0:T(8,128)S(1)}, f32[4,1,64,128]{3,2,1,0:T(8,128)S(1)}, u32[]{:S(2)}, u32[]{:S(2)}) %collective-permute-start.19) | collective-permute-done | bytes 131104 | tf_op jit(solution)/shard_map/ppermute | solution.py:18
  131.5 2.0 %collective-permute-start.20 = (f32[4,6,1,128]{3,1,2,0:T(8,128)S(1)}, f32[4,6,1,128]{3,1,2,0:T(8,128)S(1)}, u32[]{:S(2)}, u32[]{:S(2)}) collective-permute-start(f32[4,6,1,128]{3,1,2,0:T(8,128)S(1)} %copy.324), channel_id=1, source_target_pairs={{0,4},{4,8},{8,12},{12,0},{1,5},{5,9},{9,13},{13,1},{2,6},{6,10},{... | collective-permute-start | bytes 36872 | tf_op jit(solution)/shard_map/ppermute | solution.py:15
  133.5 1.7 %collective-permute-done.21 = f32[4,6,1,128]{3,1,2,0:T(8,128)S(1)} collective-permute-done((f32[4,6,1,128]{3,1,2,0:T(8,128)S(1)}, f32[4,6,1,128]{3,1,2,0:T(8,128)S(1)}, u32[]{:S(2)}, u32[]{:S(2)}) %collective-permute-start.21) | collective-permute-done | bytes 12320 | tf_op jit(solution)/shard_map/ppermute | solution.py:18
  135.3 1.9 %collective-permute-done.20 = f32[4,6,1,128]{3,1,2,0:T(8,128)S(1)} collective-permute-done((f32[4,6,1,128]{3,1,2,0:T(8,128)S(1)}, f32[4,6,1,128]{3,1,2,0:T(8,128)S(1)}, u32[]{:S(2)}, u32[]{:S(2)}) %collective-permute-start.20) | collective-permute-done | bytes 12320 | tf_op jit(solution)/shard_map/ppermute | solution.py:15
  139.1 2.8 %collective-permute-done.22 = f32[4,6,66,1]{2,1,3,0:T(8,128)S(1)} collective-permute-done((f32[4,6,66,1]{2,1,3,0:T(8,128)S(1)}, f32[4,6,66,1]{2,1,3,0:T(8,128)S(1)}, u32[]{:S(2)}, u32[]{:S(2)}) %collective-permute-start.22) | collective-permute-done | bytes 6368 | tf_op jit(solution)/shard_map/ppermute | solution.py:15
  141.9 1.3 copy.329
  143.2 1.3 copy.332
  144.7 2.4 %maximum_maximum_fusion.1 = (f32[4,6,66,129]{3,2,1,0:T(8,128)S(1)}, f32[4,6,66,129]{3,2,1,0:T(8,128)S(1)}) fusion(f32[4,6,1,128]{3,2,1,0:T(1,128)S(1)} %copy.327, f32[4,1,64,128]{3,2,1,0:T(8,128)S(1)} %collective-permute-done.19, f32[4,4,64,128]{3,2,1,0:T(8,128)S(1)} %slice_divide_fusion, f32[4,1,64,128]{3,2,1,0:T(8,128)S(1)} %collective-permute-done.18, ...), kind=kLoop, calls=%fused_computation.58 | loop fusion | flops 2043360 | bytes 2458368 | tf_op jit(solution)/shard_map/concatenate | solution.py:19
  147.4 3.2 %fusion.101 = f32[4,4,64,128]{3,2,1,0:T(8,128)} fusion(f32[4,6,66,129]{3,2,1,0:T(8,128)S(1)} %get-tuple-element.84, f32[4,6,65,128]{3,2,1,0:T(8,128)S(1)} %get-tuple-element.88, f32[4,6,66,129]{3,2,1,0:T(8,128)S(1)} %get-tuple-element.83, f32[4,1,64,128]{3,2,1,0:T(8,128)S(1)} %collective-permute-done.19, f32[4,4,64,128]{3,2,1,0:T(8,128)S(1)} %slice_divide_fusion, ...), kind=kLoop, calls=%fused_computation.220 | loop fusion | flops 7208960 | bytes 17432576 | tf_op jit(solution)/shard_map/div | solution.py:83
  (224 shorter events, 10.1 us)
Async XLA Ops:
  0.9 3.4 %copy-start.66 = (f32[4,64,128]{2,1,0:T(8,128)}, f32[4,64,128]{2,1,0:T(8,128)S(1)}, u32[]{:S(2)}) copy-start(f32[4,64,128]{2,1,0:T(8,128)S(1)} %get-tuple-element.126) | copy-start | bytes 393220
  4.6 9.5 %collective-permute-start = (f32[7,1,64,128]{3,2,1,0:T(8,128)S(1)}, f32[7,1,64,128]{3,2,1,0:T(8,128)S(1)}, u32[]{:S(2)}, u32[]{:S(2)}) collective-permute-start(f32[7,1,64,128]{3,2,1,0:T(8,128)S(1)} %get-tuple-element.77), channel_id=1, source_target_pairs={{0,16},{16,0},{1,17},{17,1},{2,18},{18,2},{3,19},{19,3},{4,20},{20... | collective-permute-start | bytes 688136 | tf_op jit(solution)/shard_map/ppermute | solution.py:15
  7.6 10.5 %collective-permute-start.1 = (f32[7,1,64,128]{3,2,1,0:T(8,128)S(1)}, f32[7,1,64,128]{3,2,1,0:T(8,128)S(1)}, u32[]{:S(2)}, u32[]{:S(2)}) collective-permute-start(f32[7,1,64,128]{3,2,1,0:T(8,128)S(1)} %get-tuple-element.78), channel_id=1, source_target_pairs={{16,0},{0,16},{17,1},{1,17},{18,2},{2,18},{19,3},{3,19},{20,4},{4,... | collective-permute-start | bytes 688136 | tf_op jit(solution)/shard_map/ppermute | solution.py:18
  18.3 5.4 %collective-permute-start.3 = (f32[7,6,1,128]{3,0,2,1:T(8,128)S(1)}, f32[7,6,1,128]{3,0,2,1:T(8,128)S(1)}, u32[]{:S(2)}, u32[]{:S(2)}) collective-permute-start(f32[7,6,1,128]{3,0,2,1:T(8,128)S(1)} %copy.335), channel_id=1, source_target_pairs={{4,0},{8,4},{12,8},{0,12},{5,1},{9,5},{13,9},{1,13},{6,2},{10,6},{... | collective-permute-start | bytes 64520 | tf_op jit(solution)/shard_map/ppermute | solution.py:18
  22.2 5.6 %collective-permute-start.2 = (f32[7,6,1,128]{3,0,2,1:T(8,128)S(1)}, f32[7,6,1,128]{3,0,2,1:T(8,128)S(1)}, u32[]{:S(2)}, u32[]{:S(2)}) collective-permute-start(f32[7,6,1,128]{3,0,2,1:T(8,128)S(1)} %copy.334), channel_id=1, source_target_pairs={{0,4},{4,8},{8,12},{12,0},{1,5},{5,9},{9,13},{13,1},{2,6},{6,10},{... | collective-permute-start | bytes 64520 | tf_op jit(solution)/shard_map/ppermute | solution.py:15
  22.5 5.4 %copy-start.10 = (f32[7,5,64,128]{3,2,1,0:T(8,128)}, f32[7,5,64,128]{3,2,1,0:T(8,128)S(1)}, u32[]{:S(2)}) copy-start(f32[7,5,64,128]{3,2,1,0:T(8,128)S(1)} %get-tuple-element.76) | copy-start | bytes 3440644
  22.5 5.4 %copy-start.8 = (f32[7,5,64,128]{3,2,1,0:T(8,128)}, f32[7,5,64,128]{3,2,1,0:T(8,128)S(1)}, u32[]{:S(2)}) copy-start(f32[7,5,64,128]{3,2,1,0:T(8,128)S(1)} %get-tuple-element.75) | copy-start | bytes 3440644
  32.9 6.5 %collective-permute-start.5 = (f32[7,6,66,1]{2,0,3,1:T(8,128)S(1)}, f32[7,6,66,1]{2,0,3,1:T(8,128)S(1)}, u32[]{:S(2)}, u32[]{:S(2)}) collective-permute-start(f32[7,6,66,1]{2,0,3,1:T(8,128)S(1)} %copy.301), channel_id=1, source_target_pairs={{0,1},{1,2},{2,3},{3,0},{4,5},{5,6},{6,7},{7,4},{8,9},{9,10},{10,1... | collective-permute-start | bytes 33272 | tf_op jit(solution)/shard_map/ppermute | solution.py:15
  33.0 4.0 %collective-permute-start.4 = (f32[7,6,66,1]{2,0,3,1:T(8,128)}, f32[7,6,66,1]{2,0,3,1:T(8,128)}, u32[]{:S(2)}, u32[]{:S(2)}) collective-permute-start(f32[7,6,66,1]{2,0,3,1:T(8,128)} %copy.298), channel_id=1, source_target_pairs={{1,0},{2,1},{3,2},{0,3},{5,4},{6,5},{7,6},{4,7},{9,8},{10,9},{11,1... | collective-permute-start | bytes 33272 | tf_op jit(solution)/shard_map/ppermute | solution.py:18
  52.6 6.2 %collective-permute-start.6 = (f32[4,1,64,128]{3,2,1,0:T(8,128)S(1)}, f32[4,1,64,128]{3,2,1,0:T(8,128)S(1)}, u32[]{:S(2)}, u32[]{:S(2)}) collective-permute-start(f32[4,1,64,128]{3,2,1,0:T(8,128)S(1)} %get-tuple-element.97), channel_id=1, source_target_pairs={{0,16},{16,0},{1,17},{17,1},{2,18},{18,2},{3,19},{19,3},{4,20},{20... | collective-permute-start | bytes 393224 | tf_op jit(solution)/shard_map/ppermute | solution.py:15
  54.2 7.5 %collective-permute-start.7 = (f32[4,1,64,128]{3,2,1,0:T(8,128)S(1)}, f32[4,1,64,128]{3,2,1,0:T(8,128)S(1)}, u32[]{:S(2)}, u32[]{:S(2)}) collective-permute-start(f32[4,1,64,128]{3,2,1,0:T(8,128)S(1)} %get-tuple-element.98), channel_id=1, source_target_pairs={{16,0},{0,16},{17,1},{1,17},{18,2},{2,18},{19,3},{3,19},{20,4},{4,... | collective-permute-start | bytes 393224 | tf_op jit(solution)/shard_map/ppermute | solution.py:18
  61.7 3.8 %collective-permute-start.9 = (f32[4,6,1,128]{3,1,2,0:T(8,128)S(1)}, f32[4,6,1,128]{3,1,2,0:T(8,128)S(1)}, u32[]{:S(2)}, u32[]{:S(2)}) collective-permute-start(f32[4,6,1,128]{3,1,2,0:T(8,128)S(1)} %copy.305), channel_id=1, source_target_pairs={{4,0},{8,4},{12,8},{0,12},{5,1},{9,5},{13,9},{1,13},{6,2},{10,6},{... | collective-permute-start | bytes 36872 | tf_op jit(solution)/shard_map/ppermute | solution.py:18
  61.8 5.6 %collective-permute-start.8 = (f32[4,6,1,128]{3,1,2,0:T(8,128)S(1)}, f32[4,6,1,128]{3,1,2,0:T(8,128)S(1)}, u32[]{:S(2)}, u32[]{:S(2)}) collective-permute-start(f32[4,6,1,128]{3,1,2,0:T(8,128)S(1)} %copy.304), channel_id=1, source_target_pairs={{0,4},{4,8},{8,12},{12,0},{1,5},{5,9},{9,13},{13,1},{2,6},{6,10},{... | collective-permute-start | bytes 36872 | tf_op jit(solution)/shard_map/ppermute | solution.py:15
  68.6 4.8 %collective-permute-start.11 = (f32[4,6,66,1]{2,1,3,0:T(8,128)S(1)}, f32[4,6,66,1]{2,1,3,0:T(8,128)S(1)}, u32[]{:S(2)}, u32[]{:S(2)}) collective-permute-start(f32[4,6,66,1]{2,1,3,0:T(8,128)S(1)} %copy.311), channel_id=1, source_target_pairs={{1,0},{2,1},{3,2},{0,3},{5,4},{6,5},{7,6},{4,7},{9,8},{10,9},{11,1... | collective-permute-start | bytes 19016 | tf_op jit(solution)/shard_map/ppermute | solution.py:18
  68.7 3.4 %collective-permute-start.10 = (f32[4,6,66,1]{2,1,3,0:T(8,128)S(1)}, f32[4,6,66,1]{2,1,3,0:T(8,128)S(1)}, u32[]{:S(2)}, u32[]{:S(2)}) collective-permute-start(f32[4,6,66,1]{2,1,3,0:T(8,128)S(1)} %copy.308), channel_id=1, source_target_pairs={{0,1},{1,2},{2,3},{3,0},{4,5},{5,6},{6,7},{7,4},{8,9},{9,10},{10,1... | collective-permute-start | bytes 19016 | tf_op jit(solution)/shard_map/ppermute | solution.py:15
  74.7 2.7 %copy-start.16 = (f32[4,64,128]{2,1,0:T(8,128)S(1)}, f32[4,64,128]{2,1,0:T(8,128)}, u32[]{:S(2)}) copy-start(f32[4,64,128]{2,1,0:T(8,128)} %get-tuple-element.101) | copy-start | bytes 393220
  74.7 2.7 %copy-start.18 = (f32[4,64,128]{2,1,0:T(8,128)S(1)}, f32[4,64,128]{2,1,0:T(8,128)}, u32[]{:S(2)}) copy-start(f32[4,64,128]{2,1,0:T(8,128)} %get-tuple-element.102) | copy-start | bytes 393220
  74.7 2.7 %copy-start.20 = (f32[4,64,128]{2,1,0:T(8,128)S(1)}, f32[4,64,128]{2,1,0:T(8,128)}, u32[]{:S(2)}) copy-start(f32[4,64,128]{2,1,0:T(8,128)} %get-tuple-element.103) | copy-start | bytes 393220
  74.7 2.7 %copy-start.22 = (f32[4,64,128]{2,1,0:T(8,128)S(1)}, f32[4,64,128]{2,1,0:T(8,128)}, u32[]{:S(2)}) copy-start(f32[4,64,128]{2,1,0:T(8,128)} %get-tuple-element.104) | copy-start | bytes 393220
  74.7 2.7 %copy-start.24 = (f32[4,64,128]{2,1,0:T(8,128)S(1)}, f32[4,64,128]{2,1,0:T(8,128)}, u32[]{:S(2)}) copy-start(f32[4,64,128]{2,1,0:T(8,128)} %get-tuple-element.105) | copy-start | bytes 393220
  74.7 2.7 %copy-start.26 = (f32[4,64,128]{2,1,0:T(8,128)S(1)}, f32[4,64,128]{2,1,0:T(8,128)}, u32[]{:S(2)}) copy-start(f32[4,64,128]{2,1,0:T(8,128)} %get-tuple-element.106) | copy-start | bytes 393220
  74.7 2.7 %copy-start.28 = (f32[4,64,128]{2,1,0:T(8,128)S(1)}, f32[4,64,128]{2,1,0:T(8,128)}, u32[]{:S(2)}) copy-start(f32[4,64,128]{2,1,0:T(8,128)} %get-tuple-element.107) | copy-start | bytes 393220
  74.8 2.7 %copy-start.30 = (f32[4,64,128]{2,1,0:T(8,128)S(1)}, f32[4,64,128]{2,1,0:T(8,128)}, u32[]{:S(2)}) copy-start(f32[4,64,128]{2,1,0:T(8,128)} %get-tuple-element.108) | copy-start | bytes 393220
  74.8 2.7 %copy-start.32 = (f32[4,64,128]{2,1,0:T(8,128)S(1)}, f32[4,64,128]{2,1,0:T(8,128)}, u32[]{:S(2)}) copy-start(f32[4,64,128]{2,1,0:T(8,128)} %get-tuple-element.109) | copy-start | bytes 393220
  74.8 2.7 %copy-start.34 = (f32[4,64,128]{2,1,0:T(8,128)S(1)}, f32[4,64,128]{2,1,0:T(8,128)}, u32[]{:S(2)}) copy-start(f32[4,64,128]{2,1,0:T(8,128)} %get-tuple-element.110) | copy-start | bytes 393220
  74.8 2.7 %copy-start.36 = (f32[4,64,128]{2,1,0:T(8,128)S(1)}, f32[4,64,128]{2,1,0:T(8,128)}, u32[]{:S(2)}) copy-start(f32[4,64,128]{2,1,0:T(8,128)} %get-tuple-element.111) | copy-start | bytes 393220
  74.8 2.7 %copy-start.38 = (f32[4,64,128]{2,1,0:T(8,128)S(1)}, f32[4,64,128]{2,1,0:T(8,128)}, u32[]{:S(2)}) copy-start(f32[4,64,128]{2,1,0:T(8,128)} %get-tuple-element.112) | copy-start | bytes 393220
  74.8 2.7 %copy-start.40 = (f32[4,64,128]{2,1,0:T(8,128)S(1)}, f32[4,64,128]{2,1,0:T(8,128)}, u32[]{:S(2)}) copy-start(f32[4,64,128]{2,1,0:T(8,128)} %get-tuple-element.113) | copy-start | bytes 393220
  74.8 2.7 %copy-start.42 = (f32[4,64,128]{2,1,0:T(8,128)S(1)}, f32[4,64,128]{2,1,0:T(8,128)}, u32[]{:S(2)}) copy-start(f32[4,64,128]{2,1,0:T(8,128)} %get-tuple-element.114) | copy-start | bytes 393220
  74.8 2.7 %copy-start.44 = (f32[4,64,128]{2,1,0:T(8,128)S(1)}, f32[4,64,128]{2,1,0:T(8,128)}, u32[]{:S(2)}) copy-start(f32[4,64,128]{2,1,0:T(8,128)} %get-tuple-element.115) | copy-start | bytes 393220
  74.8 2.7 %copy-start.46 = (f32[4,64,128]{2,1,0:T(8,128)S(1)}, f32[4,64,128]{2,1,0:T(8,128)}, u32[]{:S(2)}) copy-start(f32[4,64,128]{2,1,0:T(8,128)} %get-tuple-element.116) | copy-start | bytes 393220
  74.8 2.7 %copy-start.48 = (f32[4,64,128]{2,1,0:T(8,128)S(1)}, f32[4,64,128]{2,1,0:T(8,128)}, u32[]{:S(2)}) copy-start(f32[4,64,128]{2,1,0:T(8,128)} %get-tuple-element.117) | copy-start | bytes 393220
  74.9 2.7 %copy-start.50 = (f32[4,64,128]{2,1,0:T(8,128)S(1)}, f32[4,64,128]{2,1,0:T(8,128)}, u32[]{:S(2)}) copy-start(f32[4,64,128]{2,1,0:T(8,128)} %get-tuple-element.118) | copy-start | bytes 393220
  74.9 2.7 %copy-start.52 = (f32[4,64,128]{2,1,0:T(8,128)S(1)}, f32[4,64,128]{2,1,0:T(8,128)}, u32[]{:S(2)}) copy-start(f32[4,64,128]{2,1,0:T(8,128)} %get-tuple-element.119) | copy-start | bytes 393220
  74.9 2.7 %copy-start.54 = (f32[4,64,128]{2,1,0:T(8,128)S(1)}, f32[4,64,128]{2,1,0:T(8,128)}, u32[]{:S(2)}) copy-start(f32[4,64,128]{2,1,0:T(8,128)} %get-tuple-element.120) | copy-start | bytes 393220
  74.9 2.7 %copy-start.56 = (f32[4,64,128]{2,1,0:T(8,128)S(1)}, f32[4,64,128]{2,1,0:T(8,128)}, u32[]{:S(2)}) copy-start(f32[4,64,128]{2,1,0:T(8,128)} %get-tuple-element.121) | copy-start | bytes 393220
  74.9 2.7 %copy-start.58 = (f32[4,64,128]{2,1,0:T(8,128)S(1)}, f32[4,64,128]{2,1,0:T(8,128)}, u32[]{:S(2)}) copy-start(f32[4,64,128]{2,1,0:T(8,128)} %get-tuple-element.122) | copy-start | bytes 393220
  74.9 2.7 %copy-start.60 = (f32[4,64,128]{2,1,0:T(8,128)S(1)}, f32[4,64,128]{2,1,0:T(8,128)}, u32[]{:S(2)}) copy-start(f32[4,64,128]{2,1,0:T(8,128)} %get-tuple-element.123) | copy-start | bytes 393220
  74.9 2.7 %copy-start.62 = (f32[4,64,128]{2,1,0:T(8,128)S(1)}, f32[4,64,128]{2,1,0:T(8,128)}, u32[]{:S(2)}) copy-start(f32[4,64,128]{2,1,0:T(8,128)} %add_add_fusion) | copy-start | bytes 393220
  74.9 2.7 %copy-start.64 = (f32[4,64,128]{2,1,0:T(8,128)S(1)}, f32[4,64,128]{2,1,0:T(8,128)}, u32[]{:S(2)}) copy-start(f32[4,64,128]{2,1,0:T(8,128)} %get-tuple-element.5) | copy-start | bytes 393220
  74.9 2.7 %copy-start.67 = (f32[4,64,128]{2,1,0:T(8,128)S(1)}, f32[4,64,128]{2,1,0:T(8,128)}, u32[]{:S(2)}) copy-start(f32[4,64,128]{2,1,0:T(8,128)} %copy-done.66) | copy-start | bytes 393220
  80.4 8.5 %collective-permute-start.12 = (f32[7,1,64,128]{3,2,1,0:T(8,128)S(1)}, f32[7,1,64,128]{3,2,1,0:T(8,128)S(1)}, u32[]{:S(2)}, u32[]{:S(2)}) collective-permute-start(f32[7,1,64,128]{3,2,1,0:T(8,128)S(1)} %get-tuple-element.73), channel_id=1, source_target_pairs={{0,16},{16,0},{1,17},{17,1},{2,18},{18,2},{3,19},{19,3},{4,20},{20... | collective-permute-start | bytes 688136 | tf_op jit(solution)/shard_map/ppermute | solution.py:15
  81.9 9.7 %collective-permute-start.13 = (f32[7,1,64,128]{3,2,1,0:T(8,128)S(1)}, f32[7,1,64,128]{3,2,1,0:T(8,128)S(1)}, u32[]{:S(2)}, u32[]{:S(2)}) collective-permute-start(f32[7,1,64,128]{3,2,1,0:T(8,128)S(1)} %get-tuple-element.74), channel_id=1, source_target_pairs={{16,0},{0,16},{17,1},{1,17},{18,2},{2,18},{19,3},{3,19},{20,4},{4,... | collective-permute-start | bytes 688136 | tf_op jit(solution)/shard_map/ppermute | solution.py:18
  91.7 3.9 %collective-permute-start.15 = (f32[7,6,1,128]{3,0,2,1:T(8,128)S(1)}, f32[7,6,1,128]{3,0,2,1:T(8,128)S(1)}, u32[]{:S(2)}, u32[]{:S(2)}) collective-permute-start(f32[7,6,1,128]{3,0,2,1:T(8,128)S(1)} %copy.337), channel_id=1, source_target_pairs={{4,0},{8,4},{12,8},{0,12},{5,1},{9,5},{13,9},{1,13},{6,2},{10,6},{... | collective-permute-start | bytes 64520 | tf_op jit(solution)/shard_map/ppermute | solution.py:18
  92.0 5.6 %collective-permute-start.14 = (f32[7,6,1,128]{3,0,2,1:T(8,128)S(1)}, f32[7,6,1,128]{3,0,2,1:T(8,128)S(1)}, u32[]{:S(2)}, u32[]{:S(2)}) collective-permute-start(f32[7,6,1,128]{3,0,2,1:T(8,128)S(1)} %copy.336), channel_id=1, source_target_pairs={{0,4},{4,8},{8,12},{12,0},{1,5},{5,9},{9,13},{13,1},{2,6},{6,10},{... | collective-permute-start | bytes 64520 | tf_op jit(solution)/shard_map/ppermute | solution.py:15
  94.1 3.5 %copy-start.6 = (f32[7,5,64,128]{3,2,1,0:T(8,128)}, f32[7,5,64,128]{3,2,1,0:T(8,128)S(1)}, u32[]{:S(2)}) copy-start(f32[7,5,64,128]{3,2,1,0:T(8,128)S(1)} %get-tuple-element.72) | copy-start | bytes 3440644
  94.1 3.5 %copy-start.4 = (f32[7,5,64,128]{3,2,1,0:T(8,128)}, f32[7,5,64,128]{3,2,1,0:T(8,128)S(1)}, u32[]{:S(2)}) copy-start(f32[7,5,64,128]{3,2,1,0:T(8,128)S(1)} %get-tuple-element.71) | copy-start | bytes 3440644
  102.7 6.5 %collective-permute-start.17 = (f32[7,6,66,1]{2,0,3,1:T(8,128)S(1)}, f32[7,6,66,1]{2,0,3,1:T(8,128)S(1)}, u32[]{:S(2)}, u32[]{:S(2)}) collective-permute-start(f32[7,6,66,1]{2,0,3,1:T(8,128)S(1)} %copy.321), channel_id=1, source_target_pairs={{0,1},{1,2},{2,3},{3,0},{4,5},{5,6},{6,7},{7,4},{8,9},{9,10},{10,1... | collective-permute-start | bytes 33272 | tf_op jit(solution)/shard_map/ppermute | solution.py:15
  102.7 4.0 %collective-permute-start.16 = (f32[7,6,66,1]{2,0,3,1:T(8,128)}, f32[7,6,66,1]{2,0,3,1:T(8,128)}, u32[]{:S(2)}, u32[]{:S(2)}) collective-permute-start(f32[7,6,66,1]{2,0,3,1:T(8,128)} %copy.318), channel_id=1, source_target_pairs={{1,0},{2,1},{3,2},{0,3},{5,4},{6,5},{7,6},{4,7},{9,8},{10,9},{11,1... | collective-permute-start | bytes 33272 | tf_op jit(solution)/shard_map/ppermute | solution.py:18
  122.4 6.4 %collective-permute-start.18 = (f32[4,1,64,128]{3,2,1,0:T(8,128)S(1)}, f32[4,1,64,128]{3,2,1,0:T(8,128)S(1)}, u32[]{:S(2)}, u32[]{:S(2)}) collective-permute-start(f32[4,1,64,128]{3,2,1,0:T(8,128)S(1)} %get-tuple-element.95), channel_id=1, source_target_pairs={{0,16},{16,0},{1,17},{17,1},{2,18},{18,2},{3,19},{19,3},{4,20},{20... | collective-permute-start | bytes 393224 | tf_op jit(solution)/shard_map/ppermute | solution.py:15
  124.0 7.4 %collective-permute-start.19 = (f32[4,1,64,128]{3,2,1,0:T(8,128)S(1)}, f32[4,1,64,128]{3,2,1,0:T(8,128)S(1)}, u32[]{:S(2)}, u32[]{:S(2)}) collective-permute-start(f32[4,1,64,128]{3,2,1,0:T(8,128)S(1)} %get-tuple-element.96), channel_id=1, source_target_pairs={{16,0},{0,16},{17,1},{1,17},{18,2},{2,18},{19,3},{3,19},{20,4},{4,... | collective-permute-start | bytes 393224 | tf_op jit(solution)/shard_map/ppermute | solution.py:18
  131.5 3.8 %collective-permute-start.21 = (f32[4,6,1,128]{3,1,2,0:T(8,128)S(1)}, f32[4,6,1,128]{3,1,2,0:T(8,128)S(1)}, u32[]{:S(2)}, u32[]{:S(2)}) collective-permute-start(f32[4,6,1,128]{3,1,2,0:T(8,128)S(1)} %copy.325), channel_id=1, source_target_pairs={{4,0},{8,4},{12,8},{0,12},{5,1},{9,5},{13,9},{1,13},{6,2},{10,6},{... | collective-permute-start | bytes 36872 | tf_op jit(solution)/shard_map/ppermute | solution.py:18
  131.5 5.6 %collective-permute-start.20 = (f32[4,6,1,128]{3,1,2,0:T(8,128)S(1)}, f32[4,6,1,128]{3,1,2,0:T(8,128)S(1)}, u32[]{:S(2)}, u32[]{:S(2)}) collective-permute-start(f32[4,6,1,128]{3,1,2,0:T(8,128)S(1)} %copy.324), channel_id=1, source_target_pairs={{0,4},{4,8},{8,12},{12,0},{1,5},{5,9},{9,13},{13,1},{2,6},{6,10},{... | collective-permute-start | bytes 36872 | tf_op jit(solution)/shard_map/ppermute | solution.py:15
  138.4 4.8 %collective-permute-start.23 = (f32[4,6,66,1]{2,1,3,0:T(8,128)S(1)}, f32[4,6,66,1]{2,1,3,0:T(8,128)S(1)}, u32[]{:S(2)}, u32[]{:S(2)}) collective-permute-start(f32[4,6,66,1]{2,1,3,0:T(8,128)S(1)} %copy.331), channel_id=1, source_target_pairs={{1,0},{2,1},{3,2},{0,3},{5,4},{6,5},{7,6},{4,7},{9,8},{10,9},{11,1... | collective-permute-start | bytes 19016 | tf_op jit(solution)/shard_map/ppermute | solution.py:18
  138.4 3.4 %collective-permute-start.22 = (f32[4,6,66,1]{2,1,3,0:T(8,128)S(1)}, f32[4,6,66,1]{2,1,3,0:T(8,128)S(1)}, u32[]{:S(2)}, u32[]{:S(2)}) collective-permute-start(f32[4,6,66,1]{2,1,3,0:T(8,128)S(1)} %copy.328), channel_id=1, source_target_pairs={{0,1},{1,2},{2,3},{3,0},{4,5},{5,6},{6,7},{7,4},{8,9},{9,10},{10,1... | collective-permute-start | bytes 19016 | tf_op jit(solution)/shard_map/ppermute | solution.py:15
  144.5 2.7 %copy-start.21 = (f32[4,64,128]{2,1,0:T(8,128)S(1)}, f32[4,64,128]{2,1,0:T(8,128)}, u32[]{:S(2)}) copy-start(f32[4,64,128]{2,1,0:T(8,128)} %get-tuple-element.103) | copy-start | bytes 393220
  144.5 2.7 %copy-start.23 = (f32[4,64,128]{2,1,0:T(8,128)S(1)}, f32[4,64,128]{2,1,0:T(8,128)}, u32[]{:S(2)}) copy-start(f32[4,64,128]{2,1,0:T(8,128)} %get-tuple-element.104) | copy-start | bytes 393220
  144.5 2.7 %copy-start.25 = (f32[4,64,128]{2,1,0:T(8,128)S(1)}, f32[4,64,128]{2,1,0:T(8,128)}, u32[]{:S(2)}) copy-start(f32[4,64,128]{2,1,0:T(8,128)} %get-tuple-element.105) | copy-start | bytes 393220
  144.5 2.7 %copy-start.27 = (f32[4,64,128]{2,1,0:T(8,128)S(1)}, f32[4,64,128]{2,1,0:T(8,128)}, u32[]{:S(2)}) copy-start(f32[4,64,128]{2,1,0:T(8,128)} %get-tuple-element.106) | copy-start | bytes 393220
  144.5 2.7 %copy-start.29 = (f32[4,64,128]{2,1,0:T(8,128)S(1)}, f32[4,64,128]{2,1,0:T(8,128)}, u32[]{:S(2)}) copy-start(f32[4,64,128]{2,1,0:T(8,128)} %get-tuple-element.107) | copy-start | bytes 393220
  144.6 2.7 %copy-start.31 = (f32[4,64,128]{2,1,0:T(8,128)S(1)}, f32[4,64,128]{2,1,0:T(8,128)}, u32[]{:S(2)}) copy-start(f32[4,64,128]{2,1,0:T(8,128)} %get-tuple-element.108) | copy-start | bytes 393220
  144.6 2.7 %copy-start.33 = (f32[4,64,128]{2,1,0:T(8,128)S(1)}, f32[4,64,128]{2,1,0:T(8,128)}, u32[]{:S(2)}) copy-start(f32[4,64,128]{2,1,0:T(8,128)} %get-tuple-element.109) | copy-start | bytes 393220
  144.6 2.7 %copy-start.35 = (f32[4,64,128]{2,1,0:T(8,128)S(1)}, f32[4,64,128]{2,1,0:T(8,128)}, u32[]{:S(2)}) copy-start(f32[4,64,128]{2,1,0:T(8,128)} %get-tuple-element.110) | copy-start | bytes 393220
  144.6 2.7 %copy-start.37 = (f32[4,64,128]{2,1,0:T(8,128)S(1)}, f32[4,64,128]{2,1,0:T(8,128)}, u32[]{:S(2)}) copy-start(f32[4,64,128]{2,1,0:T(8,128)} %get-tuple-element.111) | copy-start | bytes 393220
  (38 other events, 84.7 us)
where the time goes:
time: 151 us
  waiting for transfers between devices  52.8 us (35%)
  other arithmetic  41.1 us (27%)
  local copies, waits for them, and re-layouts  31.1 us (21%)
  starting transfers between devices  24.1 us (16%)
    ppermute x12, waiting for transfers between devices, extended(): lax.ppermute(lax.slice_in_dim(block, block.shape[dim] - width, None, axis...  36.6 us
    concatenate x16, other arithmetic, extended(): block = jnp.concatenate([low, block, high], axis=dim)  19.1 us
    ppermute x12, waiting for transfers between devices, extended(): lax.ppermute(lax.slice_in_dim(block, 0, width, axis=dim), axis, backward)  16.2 us
    ppermute x12, starting transfers between devices, extended(): lax.ppermute(lax.slice_in_dim(block, block.shape[dim] - width, None, axis...  14.6 us
    ppermute x12, starting transfers between devices, extended(): lax.ppermute(lax.slice_in_dim(block, 0, width, axis=dim), axis, backward)  9.48 us
    slice x8, local copies, waits for them, and re-layouts, extended(): lax.slice_in_dim(block, 0, width, axis=dim)  9.39 us
    ppermute x8, local copies, waits for them, and re-layouts, extended(): lax.ppermute(lax.slice_in_dim(block, 0, width, axis=dim), axis, backward)  7.63 us
    ppermute x8, local copies, waits for them, and re-layouts, extended(): lax.ppermute(lax.slice_in_dim(block, block.shape[dim] - width, None, axis...  6.29 us
  transfers between devices with their start and end apart: 24, of which 18 were waited for; matrix products, arithmetic and copies ran while one was open for 9% of the time, Pallas kernels for 0%

commit v1 on v0

v1 whole, which is shorter than its diff:
```python
import functools

import jax
import jax.numpy as jnp
from jax import lax
from jax.experimental import pallas as pl
from jax.experimental.pallas import tpu as pltpu
from jax.sharding import PartitionSpec as P

PASSES = 2
MESH = pl.DeviceIdType.MESH
AXES = ("gx", "gy", "gz")
SIDES = [(dx, dy) for dx in (-1, 0, 1) for dy in (-1, 0, 1) if (dx, dy) != (0, 0)]
ROWS = 8
SLOT = 8


def bit_of(active, dx, dy, dz):
    index = 9 * (dx + 1) + 3 * (dy + 1) + (dz + 1)
    return jnp.bitwise_and(active, 1 << index) != 0


def ones_in(active):
    v = active - jnp.bitwise_and(jnp.right_shift(active, 1), 0x55555555)
    v = jnp.bitwise_and(v, 0x33333333) + jnp.bitwise_and(jnp.right_shift(v, 2), 0x33333333)
    v = jnp.bitwise_and(v + jnp.right_shift(v, 4), 0x0F0F0F0F)
    v = v + jnp.right_shift(v, 8)
    v = v + jnp.right_shift(v, 16)
    return jnp.bitwise_and(v, 63)


def kernel(
    counts, fields, code, flag, bits, out,
    pull0, push0, pull1, push1, act, volume, inverse, acc, total, shifted, packed, landed,
    side_send, side_recv, act_send, act_recv, z_send, z_recv,
):
    nf, nx, ny, nz = fields.shape
    place = [lax.axis_index(name) for name in AXES]

    def device(dx, dy, dz):
        step = (dx, dy, dz)
        return tuple(
            lax.rem(place[d] + step[d] + counts[d], counts[d]) if step[d] else place[d]
            for d in range(3)
        )

    barrier = pltpu.get_barrier_semaphore()
    for dx, dy in SIDES:
        pl.semaphore_signal(barrier, inc=1, device_id=device(dx, dy, 0), device_id_type=MESH)
    for dz in (-1, 1):
        pl.semaphore_signal(barrier, inc=1, device_id=device(0, 0, dz), device_id_type=MESH)

    lane = lax.broadcasted_iota(jnp.int32, (ROWS, nz), 1)
    chunks = ny // ROWS

    def loop_planes(count, work):
        def step(x, carry):
            work(x)
            return carry
        lax.fori_loop(0, count, step, 0)

    def window(side, size, first):
        if side == 0:
            return pl.ds(first, size), pl.ds(first, size)
        if side > 0:
            return pl.ds(first + size - 1, 1), pl.ds(first - 1, 1)
        return pl.ds(first, 1), pl.ds(first + size, 1)

    def side_copies(ref, lead, send, recv):
        copies = []
        for k, (dx, dy) in enumerate(SIDES):
            from_x, to_x = window(dx, nx, 1)
            from_y, to_y = window(dy, ny, ROWS)
            copies.append(
                pltpu.make_async_remote_copy(
                    src_ref=ref.at[lead + (from_x, from_y)],
                    dst_ref=ref.at[lead + (to_x, to_y)],
                    send_sem=send(k),
                    recv_sem=recv(k),
                    device_id=device(dx, dy, 0),
                    device_id_type=MESH,
                )
            )
        return copies

    def z_copies(turn, rows):
        copies = []
        for k, dz in enumerate((1, -1)):
            copies.append(
                pltpu.make_async_remote_copy(
                    src_ref=packed.at[turn, k, pl.ds(0, rows)],
                    dst_ref=landed.at[turn, k, pl.ds(0, rows)],
                    send_sem=z_send.at[turn, k],
                    recv_sem=z_recv.at[turn, k],
                    device_id=device(0, 0, dz),
                    device_id_type=MESH,
                )
            )
        return copies

    def prepare(x):
        for j in range(chunks):
            rows, inner = pl.ds(ROWS * j, ROWS), pl.ds(ROWS * (j + 1), ROWS)
            kappa = code[x, rows].astype(jnp.float32) * (1.0 / 1048576.0)
            active = bits[x, rows] * flag[x, rows]
            act[x + 1, inner] = active
            pull0[0, x + 1, inner] = kappa
            for c in range(nf):
                pull0[c + 1, x + 1, inner] = kappa * fields[c, x, rows]
            others = ones_in(jnp.bitwise_and(active, ((1 << 27) - 1) ^ (1 << 13)))
            inverse[x, rows] = 1.0 / (1 + others).astype(jnp.float32)

    loop_planes(nx, prepare)
    pl.semaphore_wait(barrier, len(SIDES) + 2)
    started = []

    def pull(step):
        ref = (pull0, pull1)[step]
        target = (push0, push1)[step]
        arrays = range(nf + 1) if step == 0 else range(1, nf + 1)
        turn = 2 * step
        copies = side_copies(ref, (slice(None),), lambda k: side_send.at[turn, k], lambda k: side_recv.at[turn, k])
        if step == 0:
            copies += side_copies(act, (), lambda k: act_send.at[k], lambda k: act_recv.at[k])
        for copy in copies:
            copy.start()
        for copy in copies:
            copy.wait_recv()
        started.extend(copies)
        base = 0 if step == 0 else 1

        def sums(x, j, dzs):
            found = {}
            for dx in (-1, 0, 1):
                for dy in (-1, 0, 1):
                    rows = pl.ds(ROWS * (j + 1) - dy, ROWS)
                    active = act[x + 1 - dx, rows]
                    values = [ref[c - base, x + 1 - dx, rows] for c in arrays]
                    for dz in dzs:
                        if (dx, dy, dz) == (0, 0, 0):
                            terms = values
                        else:
                            member = bit_of(active, dx, dy, dz)
                            terms = [jnp.where(member, v, 0.0) for v in values]
                        if dz in found:
                            found[dz] = [a + b for a, b in zip(found[dz], terms)]
                        else:
                            found[dz] = terms
            return found

        def outer(x):
            for j in range(chunks):
                found = sums(x, j, (1, -1))
                rows = pl.ds(ROWS * j, ROWS)
                for k, dz in enumerate((1, -1)):
                    tile = packed[turn, k, rows]
                    for c, value in zip(arrays, found[dz]):
                        acc[k, c, x, rows] = value
                        at = x * SLOT + c
                        amount = at + 1 if dz == 1 else at
                        tile = jnp.where(lane == at, pltpu.roll(value, amount, 1), tile)
                    packed[turn, k, rows] = tile

        packed[turn] = jnp.zeros_like(packed[turn])
        loop_planes(nx, outer)
        copies = z_copies(turn, ny)
        for copy in copies:
            copy.start()
        started.extend(copies)

        def middle(x):
            for j in range(chunks):
                for c, value in zip(arrays, sums(x, j, (0,))[0]):
                    total[c, x, pl.ds(ROWS * j, ROWS)] = value

        loop_planes(nx, middle)
        for copy in copies:
            copy.wait_recv()

        def finish(x):
            for j in range(chunks):
                rows, inner = pl.ds(ROWS * j, ROWS), pl.ds(ROWS * (j + 1), ROWS)
                low, high = landed[turn, 0, rows], landed[turn, 1, rows]
                found = {}
                for c in arrays:
                    at = x * SLOT + c
                    from_low = jnp.where(
                        lane == 0, pltpu.roll(low, nz - at, 1), pltpu.roll(acc[0, c, x, rows], 1, 1)
                    )
                    from_high = jnp.where(
                        lane == nz - 1,
                        pltpu.roll(high, nz - 1 - at, 1),
                        pltpu.roll(acc[1, c, x, rows], nz - 1, 1),
                    )
                    found[c] = total[c, x, rows] + from_low + from_high
                if step == 0:
                    scale = 1.0 / found[0]
                    volume[x, rows] = scale
                else:
                    scale = volume[x, rows]
                for c in range(nf):
                    target[c, x + 1, inner] = found[c + 1] * scale

        loop_planes(nx, finish)

    def push(step):
        ref = (push0, push1)[step]
        turn = 2 * step + 1
        copies = side_copies(ref, (slice(None),), lambda k: side_send.at[turn, k], lambda k: side_recv.at[turn, k])
        for copy in copies:
            copy.start()
        for copy in copies:
            copy.wait_recv()
        started.extend(copies)

        def columns(x):
            for j in range(chunks + 2):
                rows = pl.ds(ROWS * j, ROWS)
                for k, dz in enumerate((1, -1)):
                    tile = packed[turn, k, rows]
                    for c in range(nf):
                        at = x * SLOT + c
                        amount = at + 1 if dz == 1 else at
                        tile = jnp.where(lane == at, pltpu.roll(ref[c, x, rows], amount, 1), tile)
                    packed[turn, k, rows] = tile

        packed[turn] = jnp.zeros_like(packed[turn])
        loop_planes(nx + 2, columns)
        copies = z_copies(turn, ny + 2 * ROWS)
        for copy in copies:
            copy.start()
        started.extend(copies)

        def gathered(x, j, dz, read, values, active):
            for dx in (-1, 0, 1):
                for dy in (-1, 0, 1):
                    rows = pl.ds(ROWS * (j + 1) + dy, ROWS)
                    terms = [read(c, x + 1 + dx, rows) for c in range(nf)]
                    if (dx, dy, dz) != (0, 0, 0):
                        member = bit_of(active, dx, dy, dz)
                        terms = [jnp.where(member, v, 0.0) for v in terms]
                    values = terms if values is None else [a + b for a, b in zip(values, terms)]
            return values

        def middle(x):
            for j in range(chunks):
                active = act[x + 1, pl.ds(ROWS * (j + 1), ROWS)]
                values = gathered(x, j, 0, lambda c, at, rows: ref[c, at, rows], None, active)
                for c in range(nf):
                    total[c, x, pl.ds(ROWS * j, ROWS)] = values[c]

        loop_planes(nx, middle)
        for copy in copies:
            copy.wait_recv()

        def shift(x):
            for j in range(chunks + 2):
                rows = pl.ds(ROWS * j, ROWS)
                low, high = landed[turn, 0, rows], landed[turn, 1, rows]
                for c in range(nf):
                    at = x * SLOT + c
                    value = ref[c, x, rows]
                    shifted[0, c, x, rows] = jnp.where(
                        lane == 0, pltpu.roll(low, nz - at, 1), pltpu.roll(value, 1, 1)
                    )
                    shifted[1, c, x, rows] = jnp.where(
                        lane == nz - 1, pltpu.roll(high, nz - 1 - at, 1), pltpu.roll(value, nz - 1, 1)
                    )

        loop_planes(nx + 2, shift)

        def finish(x):
            for j in range(chunks):
                rows, inner = pl.ds(ROWS * j, ROWS), pl.ds(ROWS * (j + 1), ROWS)
                active = act[x + 1, inner]
                values = [total[c, x, rows] for c in range(nf)]
                for k, dz in ((0, -1), (1, 1)):
                    values = gathered(x, j, dz, lambda c, at, r: shifted[k, c, at, r], values, active)
                scale = inverse[x, rows]
                if step == PASSES - 1:
                    for c in range(nf):
                        out[c, x, rows] = values[c] * scale
                else:
                    scale = scale * pull0[0, x + 1, inner]
                    for c in range(nf):
                        pull1[c, x + 1, inner] = values[c] * scale

        loop_planes(nx, finish)

    for step in range(PASSES):
        pull(step)
        push(step)
    for copy in started:
        copy.wait_send()


def body(counts, fields, code, flag, bits):
    nf, nx, ny, nz = fields.shape
    frame = (nx + 2, ny + 2 * ROWS, nz)
    turns = 2 * PASSES
    vmem = pl.BlockSpec(memory_space=pltpu.VMEM)
    f32 = jnp.float32
    return pl.pallas_call(
        functools.partial(kernel, counts),
        out_shape=jax.ShapeDtypeStruct(fields.shape, f32),
        in_specs=[vmem] * 4,
        out_specs=vmem,
        scratch_shapes=[
            pltpu.VMEM((nf + 1,) + frame, f32),
            pltpu.VMEM((nf,) + frame, f32),
            pltpu.VMEM((nf,) + frame, f32),
            pltpu.VMEM((nf,) + frame, f32),
            pltpu.VMEM(frame, jnp.int32),
            pltpu.VMEM((nx, ny, nz), f32),
            pltpu.VMEM((nx, ny, nz), f32),
            pltpu.VMEM((2, nf + 1, nx, ny, nz), f32),
            pltpu.VMEM((nf + 1, nx, ny, nz), f32),
            pltpu.VMEM((2, nf) + frame, f32),
            pltpu.VMEM((turns, 2, ny + 2 * ROWS, nz), f32),
            pltpu.VMEM((turns, 2, ny + 2 * ROWS, nz), f32),
            pltpu.SemaphoreType.DMA((turns, len(SIDES))),
            pltpu.SemaphoreType.DMA((turns, len(SIDES))),
            pltpu.SemaphoreType.DMA((len(SIDES),)),
            pltpu.SemaphoreType.DMA((len(SIDES),)),
            pltpu.SemaphoreType.DMA((turns, 2)),
            pltpu.SemaphoreType.DMA((turns, 2)),
        ],
        compiler_params=pltpu.CompilerParams(collective_id=0, has_side_effects=True),
    )(fields, code, flag, bits)


def solution(mesh):
    counts = tuple(mesh.shape[name] for name in AXES)
    spec = P("gx", "gy", "gz")
    whole = P(None, "gx", "gy", "gz")
    return jax.shard_map(
        functools.partial(body, counts),
        mesh=mesh,
        in_specs=(whole, spec, spec, spec),
        out_specs=whole,
        check_vma=False,
    )
```

time: 151 us -> 63.6 us (0.42)
  Pallas kernels: 0 us -> 61.6 us
  waiting for transfers between devices: 52.8 us -> 0 us
  other arithmetic: 41.1 us -> 0 us
  local copies, waits for them, and re-layouts: 31.1 us -> 1.89 us
  starting transfers between devices: 24.1 us -> 0 us
    pallas_call x0 -> x1, Pallas kernels: none -> 61.6 us  [body(): pl.pallas_call(functools.partial(kernel, counts), out_shape=jax.ShapeDtyp...]
    ppermute x24 -> x0, waiting for transfers between devices: 52.8 us -> none  [the longest x12 36.6 us: extended(): lax.ppermute(lax.slice_in_dim(block, block.shape[dim] - width, None, axis...]
    ppermute x24 -> x0, starting transfers between devices: 24.1 us -> none  [the longest x12 14.6 us: extended(): lax.ppermute(lax.slice_in_dim(block, block.shape[dim] - width, None, axis...]
    concatenate x18 -> x0, other arithmetic: 19.2 us -> none  [the longest x16 19.1 us: extended(): block = jnp.concatenate([low, block, high], axis=dim)]
    ppermute x16 -> x0, local copies, waits for them, and re-layouts: 13.9 us -> none  [the longest x8 7.63 us: extended(): lax.ppermute(lax.slice_in_dim(block, 0, width, axis=dim), axis, backward)]
    slice x22 -> x0, local copies, waits for them, and re-layouts: 12.2 us -> none  [the longest x8 9.39 us: extended(): lax.slice_in_dim(block, 0, width, axis=dim)]
    mul x11 -> x0, other arithmetic: 7.17 us -> none  [the longest x9 4.53 us: pulled_sums(): sums = sums + member[None] * piece[:5]]
    add x3 -> x0, other arithmetic: 6.96 us -> none  [the longest x2 5.84 us: pulled_sums(): sums = sums + member[None] * piece[:5]]
  transfers between devices with their start and end apart: 24 -> 0, of which waited for: 18 -> 0; matrix products, arithmetic and copies ran while one was open for 9% -> 0% of each run, Pallas kernels for 0% -> 0%
where the time goes in v1:
time: 63.6 us; the launch traced here: 63.5 us
  Pallas kernels  61.6 us (97%)
  local copies, waits for them, and re-layouts  1.89 us (3%)
    pallas_call x1, Pallas kernels, body(): pl.pallas_call(functools.partial(kernel, counts), out_shape=jax.ShapeDtyp...  61.6 us
    unnamed x1, local copies, waits for them, and re-layouts  1.89 us

profile of v1, /device:TPU:0, one launch (start us, length us, event | category | flops | bytes accessed | tf_op | source)
XLA Modules:
  0.0 63.5 jit_solution(14131038783498846982)
XLA Ops:
  0.0 61.6 %shard_map.46 = f32[4,4,64,128]{3,2,1,0:T(8,128)} custom-call(f32[4,4,64,128]{3,2,1,0:T(8,128)} %fields.1, s32[4,64,128]{2,1,0:T(8,128)} %code.1, s32[4,64,128]{2,1,0:T(8,128)} %flag.1, s32[4,64,128]{2,1,0:T(8,128)} %bits.1), custom_call_target="tpu_custom_call" | custom-call | tf_op jit(solution)/shard_map/pallas_call | solution.py:303
  61.6 1.9 %copy.6 = f32[4,4,64,128]{3,2,1,0:T(8,128)} copy(f32[4,4,64,128]{3,2,1,0:T(8,128)} %shard_map.46) | data formatting | bytes 1048576

commit v2 on v1

v2 whole, which is shorter than its diff:
```python
import functools

import jax
import jax.numpy as jnp
from jax import lax
from jax.experimental import pallas as pl
from jax.experimental.pallas import tpu as pltpu
from jax.sharding import PartitionSpec as P

PASSES = 2
MESH = pl.DeviceIdType.MESH
AXES = ("gx", "gy", "gz")
SIDES = [(dx, dy) for dx in (-1, 0, 1) for dy in (-1, 0, 1) if (dx, dy) != (0, 0)]
ROWS = 8
SLOT = 8


def bit_of(active, dx, dy, dz):
    index = 9 * (dx + 1) + 3 * (dy + 1) + (dz + 1)
    return jnp.bitwise_and(active, 1 << index) != 0


def ones_in(active):
    v = active - jnp.bitwise_and(jnp.right_shift(active, 1), 0x55555555)
    v = jnp.bitwise_and(v, 0x33333333) + jnp.bitwise_and(jnp.right_shift(v, 2), 0x33333333)
    v = jnp.bitwise_and(v + jnp.right_shift(v, 4), 0x0F0F0F0F)
    v = v + jnp.right_shift(v, 8)
    v = v + jnp.right_shift(v, 16)
    return jnp.bitwise_and(v, 63)


def kernel(
    counts, fields, code, flag, bits, out,
    pull0, push0, pull1, push1, act, volume, inverse, acc, total, shifted, packed, landed,
    side_send, side_recv, act_send, act_recv, z_send, z_recv,
):
    nf, nx, ny, nz = fields.shape
    place = [lax.axis_index(name) for name in AXES]

    def device(dx, dy, dz):
        step = (dx, dy, dz)
        return tuple(
            lax.rem(place[d] + step[d] + counts[d], counts[d]) if step[d] else place[d]
            for d in range(3)
        )

    barrier = pltpu.get_barrier_semaphore()
    for dx, dy in SIDES:
        pl.semaphore_signal(barrier, inc=1, device_id=device(dx, dy, 0), device_id_type=MESH)
    for dz in (-1, 1):
        pl.semaphore_signal(barrier, inc=1, device_id=device(0, 0, dz), device_id_type=MESH)

    lane = lax.broadcasted_iota(jnp.int32, (ROWS, nz), 1)
    chunks = ny // ROWS

    def loop_planes(count, work):
        def step(x, carry):
            work(x)
            return carry
        lax.fori_loop(0, count, step, 0)

    def window(side, size, first):
        if side == 0:
            return pl.ds(first, size), pl.ds(first, size)
        if side > 0:
            return pl.ds(first + size - 1, 1), pl.ds(first - 1, 1)
        return pl.ds(first, 1), pl.ds(first + size, 1)

    def side_copies(ref, lead, send, recv):
        copies = []
        for k, (dx, dy) in enumerate(SIDES):
            from_x, to_x = window(dx, nx, 1)
            from_y, to_y = window(dy, ny, ROWS)
            copies.append(
                pltpu.make_async_remote_copy(
                    src_ref=ref.at[lead + (from_x, from_y)],
                    dst_ref=ref.at[lead + (to_x, to_y)],
                    send_sem=send(k),
                    recv_sem=recv(k),
                    device_id=device(dx, dy, 0),
                    device_id_type=MESH,
                )
            )
        return copies

    def z_copies(turn, group, rows):
        copies = []
        for k, dz in enumerate((1, -1)):
            copies.append(
                pltpu.make_async_remote_copy(
                    src_ref=packed.at[turn, group, k, pl.ds(0, rows)],
                    dst_ref=landed.at[turn, group, k, pl.ds(0, rows)],
                    send_sem=z_send.at[turn, group, k],
                    recv_sem=z_recv.at[turn, group, k],
                    device_id=device(0, 0, dz),
                    device_id_type=MESH,
                )
            )
        return copies

    started = []

    def start(copies):
        for copy in copies:
            copy.start()
        started.extend(copies)

    def arrive(copies):
        for copy in copies:
            copy.wait_recv()

    def turn_copies(turn):
        ref = (pull0, push0, pull1, push1)[turn]
        copies = side_copies(
            ref, (slice(None),), lambda k: side_send.at[turn, k], lambda k: side_recv.at[turn, k]
        )
        sides = SIDES
        if turn == 0:
            copies += side_copies(act, (), lambda k: act_send.at[k], lambda k: act_recv.at[k])
            sides = SIDES + SIDES
        across = [copy for copy, side in zip(copies, sides) if side[0] != 0]
        along = [copy for copy, side in zip(copies, sides) if side[0] == 0]
        return across, along

    ends = sorted({0, nx - 1})

    def inner_planes(work):
        if nx > 2:
            def step(x, carry):
                work(x)
                return carry
            lax.fori_loop(1, nx - 1, step, 0)

    def own(x, sign):
        inside = [dx for dx in (-1, 0, 1) if 0 <= x - sign * dx < nx]
        return inside, [dx for dx in (-1, 0, 1) if dx not in inside]

    def rolled(value, amount):
        return pltpu.roll(value, amount % nz, 1)

    def prepare(x):
        for j in range(chunks):
            rows, inner = pl.ds(ROWS * j, ROWS), pl.ds(ROWS * (j + 1), ROWS)
            kappa = code[x, rows].astype(jnp.float32) * (1.0 / 1048576.0)
            active = bits[x, rows] * flag[x, rows]
            act[x + 1, inner] = active
            pull0[0, x + 1, inner] = kappa
            for c in range(nf):
                pull0[c + 1, x + 1, inner] = kappa * fields[c, x, rows]
            others = ones_in(jnp.bitwise_and(active, ((1 << 27) - 1) ^ (1 << 13)))
            inverse[x, rows] = 1.0 / (1 + others).astype(jnp.float32)

    loop_planes(nx, prepare)
    packed[...] = jnp.zeros_like(packed)
    pl.semaphore_wait(barrier, len(SIDES) + 2)
    flights = [turn_copies(turn) for turn in range(2 * PASSES)]
    start(flights[0][1])
    start(flights[0][0])

    def pull(step):
        ref = (pull0, pull1)[step]
        target = (push0, push1)[step]
        arrays = range(nf + 1) if step == 0 else range(1, nf + 1)
        turn = 2 * step
        base = 0 if step == 0 else 1
        across, along = flights[turn]

        def sums(x, j, dxs, dzs, found):
            for dx in dxs:
                for dy in (-1, 0, 1):
                    rows = pl.ds(ROWS * (j + 1) - dy, ROWS)
                    active = act[x + 1 - dx, rows]
                    values = [ref[c - base, x + 1 - dx, rows] for c in arrays]
                    for dz in dzs:
                        if (dx, dy, dz) == (0, 0, 0):
                            terms = values
                        else:
                            member = bit_of(active, dx, dy, dz)
                            terms = [jnp.where(member, v, 0.0) for v in values]
                        if dz in found:
                            found[dz] = [a + b for a, b in zip(found[dz], terms)]
                        else:
                            found[dz] = terms
            return found

        def pack(x, j, found):
            rows = pl.ds(ROWS * j, ROWS)
            for k, dz in enumerate((1, -1)):
                tile = packed[turn, 0, k, rows]
                for c, value in zip(arrays, found[dz]):
                    acc[k, c, x, rows] = value
                    at = x * SLOT + c
                    tile = jnp.where(lane == at, rolled(value, at + (dz == 1)), tile)
                packed[turn, 0, k, rows] = tile

        def early(x, dxs, complete):
            for j in range(chunks):
                rows = pl.ds(ROWS * j, ROWS)
                found = sums(x, j, dxs, (1, 0, -1), {})
                for c, value in zip(arrays, found[0]):
                    total[c, x, rows] = value
                if complete:
                    pack(x, j, found)
                else:
                    for k, dz in enumerate((1, -1)):
                        for c, value in zip(arrays, found[dz]):
                            acc[k, c, x, rows] = value

        arrive(along)
        inner_planes(lambda x: early(x, (-1, 0, 1), True))
        for x in ends:
            early(x, own(x, 1)[0], False)
        arrive(across)
        for x in ends:
            for j in range(chunks):
                rows = pl.ds(ROWS * j, ROWS)
                found = {dz: [acc[k, c, x, rows] for c in arrays] for k, dz in enumerate((1, -1))}
                pack(x, j, sums(x, j, own(x, 1)[1], (1, -1), found))
        copies = z_copies(turn, 0, ny)
        start(copies)
        for x in ends:
            for j in range(chunks):
                rows = pl.ds(ROWS * j, ROWS)
                found = {0: [total[c, x, rows] for c in arrays]}
                for c, value in zip(arrays, sums(x, j, own(x, 1)[1], (0,), found)[0]):
                    total[c, x, rows] = value
        arrive(copies)

        def finish(x):
            for j in range(chunks):
                rows, inner = pl.ds(ROWS * j, ROWS), pl.ds(ROWS * (j + 1), ROWS)
                low, high = landed[turn, 0, 0, rows], landed[turn, 0, 1, rows]
                found = {}
                for c in arrays:
                    at = x * SLOT + c
                    from_low = jnp.where(lane == 0, rolled(low, nz - at), rolled(acc[0, c, x, rows], 1))
                    from_high = jnp.where(
                        lane == nz - 1, rolled(high, nz - 1 - at), rolled(acc[1, c, x, rows], nz - 1)
                    )
                    found[c] = total[c, x, rows] + from_low + from_high
                if step == 0:
                    scale = 1.0 / found[0]
                    volume[x, rows] = scale
                else:
                    scale = volume[x, rows]
                for c in range(nf):
                    target[c, x + 1, inner] = found[c + 1] * scale

        for x in ends:
            finish(x)
        start(flights[turn + 1][0])
        inner_planes(finish)
        start(flights[turn + 1][1])

    def push(step):
        ref = (push0, push1)[step]
        turn = 2 * step + 1
        across, along = flights[turn]

        def columns(group, x):
            for j in range(chunks + 2):
                rows = pl.ds(ROWS * j, ROWS)
                for k, dz in enumerate((1, -1)):
                    tile = packed[turn, group, k, rows]
                    for c in range(nf):
                        at = x * SLOT + c
                        tile = jnp.where(lane == at, rolled(ref[c, x, rows], at + (dz == 1)), tile)
                    packed[turn, group, k, rows] = tile

        def shift(group, x):
            for j in range(chunks + 2):
                rows = pl.ds(ROWS * j, ROWS)
                low, high = landed[turn, group, 0, rows], landed[turn, group, 1, rows]
                for c in range(nf):
                    at = x * SLOT + c
                    value = ref[c, x, rows]
                    shifted[0, c, x, rows] = jnp.where(lane == 0, rolled(low, nz - at), rolled(value, 1))
                    shifted[1, c, x, rows] = jnp.where(
                        lane == nz - 1, rolled(high, nz - 1 - at), rolled(value, nz - 1)
                    )

        def planes(first, count, work):
            def step(x, carry):
                work(x)
                return carry
            lax.fori_loop(first, first + count, step, 0)

        def gathered(x, j, dxs, dzs, values):
            active = act[x + 1, pl.ds(ROWS * (j + 1), ROWS)]
            for dz in dzs:
                for dx in dxs:
                    for dy in (-1, 0, 1):
                        rows = pl.ds(ROWS * (j + 1) + dy, ROWS)
                        if dz == 0:
                            terms = [ref[c, x + 1 + dx, rows] for c in range(nf)]
                        else:
                            terms = [shifted[(dz + 1) // 2, c, x + 1 + dx, rows] for c in range(nf)]
                        if (dx, dy, dz) != (0, 0, 0):
                            member = bit_of(active, dx, dy, dz)
                            terms = [jnp.where(member, v, 0.0) for v in terms]
                        values = terms if values is None else [a + b for a, b in zip(values, terms)]
            return values

        def held(x, j):
            return [total[c, x, pl.ds(ROWS * j, ROWS)] for c in range(nf)]

        def keep(x, j, values):
            for c in range(nf):
                total[c, x, pl.ds(ROWS * j, ROWS)] = values[c]

        def give(x, j, values):
            rows, inner = pl.ds(ROWS * j, ROWS), pl.ds(ROWS * (j + 1), ROWS)
            scale = inverse[x, rows]
            if step == PASSES - 1:
                for c in range(nf):
                    out[c, x, rows] = values[c] * scale
            else:
                scale = scale * pull0[0, x + 1, inner]
                for c in range(nf):
                    pull1[c, x + 1, inner] = values[c] * scale

        def add(x, dxs, dzs, first, last):
            for j in range(chunks):
                values = gathered(x, j, dxs, dzs, None if first else held(x, j))
                (give if last else keep)(x, j, values)

        arrive(along)
        planes(1, nx, lambda x: columns(0, x))
        copies = z_copies(turn, 0, ny + 2 * ROWS)
        start(copies)
        inner_planes(lambda x: add(x, (-1, 0, 1), (0,), True, False))
        for x in ends:
            add(x, own(x, -1)[0], (0,), True, False)
        arrive(copies)
        planes(1, nx, lambda x: shift(0, x))
        for x in ends:
            add(x, own(x, -1)[0], (-1, 1), False, False)
        inner_planes(lambda x: add(x, (-1, 0, 1), (-1, 1), False, True))
        arrive(across)
        for x in (0, nx + 1):
            columns(1, x)
        copies = z_copies(turn, 1, ny + 2 * ROWS)
        start(copies)
        for x in ends:
            add(x, own(x, -1)[1], (0,), False, False)
        arrive(copies)
        for x in (0, nx + 1):
            shift(1, x)
        for x in ends:
            add(x, own(x, -1)[1], (-1, 1), False, True)
        if step < PASSES - 1:
            start(flights[turn + 1][1])
            start(flights[turn + 1][0])

    for step in range(PASSES):
        pull(step)
        push(step)
    for copy in started:
        copy.wait_send()


def body(counts, fields, code, flag, bits):
    nf, nx, ny, nz = fields.shape
    frame = (nx + 2, ny + 2 * ROWS, nz)
    turns = 2 * PASSES
    vmem = pl.BlockSpec(memory_space=pltpu.VMEM)
    f32 = jnp.float32
    return pl.pallas_call(
        functools.partial(kernel, counts),
        out_shape=jax.ShapeDtypeStruct(fields.shape, f32),
        in_specs=[vmem] * 4,
        out_specs=vmem,
        scratch_shapes=[
            pltpu.VMEM((nf + 1,) + frame, f32),
            pltpu.VMEM((nf,) + frame, f32),
            pltpu.VMEM((nf,) + frame, f32),
            pltpu.VMEM((nf,) + frame, f32),
            pltpu.VMEM(frame, jnp.int32),
            pltpu.VMEM((nx, ny, nz), f32),
            pltpu.VMEM((nx, ny, nz), f32),
            pltpu.VMEM((2, nf + 1, nx, ny, nz), f32),
            pltpu.VMEM((nf + 1, nx, ny, nz), f32),
            pltpu.VMEM((2, nf) + frame, f32),
            pltpu.VMEM((turns, 2, 2, ny + 2 * ROWS, nz), f32),
            pltpu.VMEM((turns, 2, 2, ny + 2 * ROWS, nz), f32),
            pltpu.SemaphoreType.DMA((turns, len(SIDES))),
            pltpu.SemaphoreType.DMA((turns, len(SIDES))),
            pltpu.SemaphoreType.DMA((len(SIDES),)),
            pltpu.SemaphoreType.DMA((len(SIDES),)),
            pltpu.SemaphoreType.DMA((turns, 2, 2)),
            pltpu.SemaphoreType.DMA((turns, 2, 2)),
        ],
        compiler_params=pltpu.CompilerParams(collective_id=0, has_side_effects=True),
    )(fields, code, flag, bits)


def solution(mesh):
    counts = tuple(mesh.shape[name] for name in AXES)
    spec = P("gx", "gy", "gz")
    whole = P(None, "gx", "gy", "gz")
    return jax.shard_map(
        functools.partial(body, counts),
        mesh=mesh,
        in_specs=(whole, spec, spec, spec),
        out_specs=whole,
        check_vma=False,
    )
```

time: 63.6 us -> 59.3 us (0.932)
  Pallas kernels: 61.6 us -> 57.2 us
    pallas_call x1, Pallas kernels: 61.6 us -> 57.2 us  [body(): pl.pallas_call(functools.partial(kernel, counts), out_shape=jax.ShapeDtyp...]
where the time goes in v2:
time: 59.3 us; the launch traced here: 59.1 us
  Pallas kernels  57.2 us (96%)
  local copies, waits for them, and re-layouts  1.89 us (3%)
    pallas_call x1, Pallas kernels, body(): pl.pallas_call(functools.partial(kernel, counts), out_shape=jax.ShapeDtyp...  57.2 us
    unnamed x1, local copies, waits for them, and re-layouts  1.89 us

profile of v2, /device:TPU:0, one launch (start us, length us, event | category | flops | bytes accessed | tf_op | source)
XLA Modules:
  0.0 59.1 jit_solution(15160597334326769220)
XLA Ops:
  0.0 57.2 %shard_map.46 = f32[4,4,64,128]{3,2,1,0:T(8,128)} custom-call(f32[4,4,64,128]{3,2,1,0:T(8,128)} %fields.1, s32[4,64,128]{2,1,0:T(8,128)} %code.1, s32[4,64,128]{2,1,0:T(8,128)} %flag.1, s32[4,64,128]{2,1,0:T(8,128)} %bits.1), custom_call_target="tpu_custom_call" | custom-call | tf_op jit(solution)/shard_map/pallas_call | solution.py:368
  57.2 1.9 %copy.6 = f32[4,4,64,128]{3,2,1,0:T(8,128)} copy(f32[4,4,64,128]{3,2,1,0:T(8,128)} %shard_map.46) | data formatting | bytes 1048576
